TPU v7x, 256 devices: a whole 4x4x8 slice. The times are simulated.
256 devices in a mesh: row: 8 (over x, y_lo), col: 32 (over z, y_hi, core).
Axes of the slice: x: 4, y: 4 (y_hi: 2, y_lo: 2; y = y_hi * 2 + y_lo), z: 8, core: 2. Of those that a mesh axis runs over, the one named last changes fastest.
Arguments:
- grad_out: bfloat16 [2048, 8192], P('col', 'row'), may hold values from -6 to 6
- weight: bfloat16 [28672, 8192], P('col', 'row'), may hold values from -0.0625 to 0.0625
Outputs:
- grad_in: bfloat16 [2048, 28672], P('row', 'col')
All inputs are finite; a program needn't handle non-finite values.
Results may differ from a plain program's by a relative error of at most 0.001.
Values may be sent and summed in bfloat16 or wider, within the bound.
A program may use at most 64 MiB of HBM per device.

v0:
```python
import jax
import jax.numpy as jnp
from jax import lax
from jax.sharding import Mesh
from jax.sharding import PartitionSpec as P

ROW = ("row_0", "row_1")


def scatter_axes(array, axes, dim):
    if not axes:
        return array
    nearer = lax.psum_scatter(array, axes[0], scatter_dimension=dim, tiled=True)
    return scatter_axes(nearer, axes[1:], dim)


def contract(rows_block, weight):
    return lax.dot_general(
        rows_block, weight, (((1,), (1,)), ((), ())), preferred_element_type=jnp.float32
    )


def local(grad_out, weight):
    partial_value = contract(lax.all_gather(grad_out, "col", axis=0, tiled=True), weight)
    return scatter_axes(partial_value, ROW, 0).astype(jnp.bfloat16)


def solution(mesh):
    finer = Mesh(mesh.devices.reshape(4, 2, mesh.shape["col"]), ("row_0", "row_1", "col"))
    in_specs = (P("col", ROW), P("col", ROW))
    out_specs = P(ROW, "col")
    return jax.shard_map(local, mesh=finer, in_specs=in_specs, out_specs=out_specs, check_vma=False)
```

profile of v0, /device:TPU:1, one launch (start us, length us, event | category | flops | bytes accessed | tf_op | source)
XLA Modules:
  0.0 226.0 jit_solution(12876038008683448927)
XLA Ops:
  6.5 0.0 copy-start
  6.5 0.0 all-gather.2.cloned.1.call-start
  6.5 0.7 all-gather.2.cloned.1.call-update
  7.3 0.0 reduce-scatter.3.cloned.1.call-start
  7.3 93.6 %all-gather.2.cloned.1.call-done = bf16[2048,1024]{1,0:T(8,128)(2,1)} async-done(((bf16[64,1024]{1,0:T(8,128)(2,1)}), bf16[2048,1024]{1,0:T(8,128)(2,1)}) %all-gather.2.cloned.1.call-update) | async-done | bytes 4194320 | tf_op jit(solution)/shard_map/all_gather | solution.py:24
  100.9 0.0 copy-done
  100.9 8.8 %fusion = f32[2048,896]{1,0:T(8,128)} fusion(bf16[2048,1024]{1,0:T(8,128)(2,1)} %all-gather.2.cloned.1.call-done, bf16[896,1024]{1,0:T(8,128)(2,1)S(1)} %copy-done), kind=kOutput, calls=%fused_computation | convolution fusion | flops 3758096384 | bytes 13369344 | tf_op jit(solution)/shard_map/dot_general | solution.py:18
  109.7 0.0 reduce-scatter.3.cloned.1.call-update
  109.7 0.0 reduce-scatter.5.cloned.1.call-start
  109.7 71.4 %reduce-scatter.3.cloned.1.call-done = f32[512,896]{1,0:T(8,128)} async-done(((f32[2048,896]{1,0:T(8,128)}), f32[512,896]{1,0:T(8,128)}) %reduce-scatter.3.cloned.1.call-update) | async-done | bytes 1835024 | tf_op jit(solution)/shard_map/reduce_scatter | solution.py:13
  181.2 0.0 reduce-scatter.5.cloned.1.call-update
  181.2 36.3 %reduce-scatter.5.cloned.1.call-done = f32[256,896]{1,0:T(8,128)} async-done(((f32[512,896]{1,0:T(8,128)}), f32[256,896]{1,0:T(8,128)}) %reduce-scatter.5.cloned.1.call-update) | async-done | bytes 917520 | tf_op jit(solution)/shard_map/reduce_scatter | solution.py:13
  217.5 2.0 convert_element_type.3
Async XLA Ops:
  6.5 94.4 %copy-start = (bf16[896,1024]{1,0:T(8,128)(2,1)S(1)}, bf16[896,1024]{1,0:T(8,128)(2,1)}, u32[]{:S(2)}) copy-start(bf16[896,1024]{1,0:T(8,128)(2,1)} %param.3) | copy-start | bytes 5505028
  6.5 94.4 %all-gather.2.cloned.1.call-start = ((), (), s32[]{:S(2)}) async-start(), calls=%async_computation.2 | async-start | bytes 4325376 | tf_op jit(solution)/shard_map/all_gather | solution.py:24
  7.3 173.9 %reduce-scatter.3.cloned.1.call-start = ((), (), s32[]{:S(2)}) async-start(), calls=%async_computation.3 | async-start | bytes 9175040 | tf_op jit(solution)/shard_map/reduce_scatter | solution.py:13
  109.7 107.8 %reduce-scatter.5.cloned.1.call-start = ((), (), s32[]{:S(2)}) async-start(), calls=%async_computation.4 | async-start | bytes 2752512 | tf_op jit(solution)/shard_map/reduce_scatter | solution.py:13
Sparse Core Ops, SparseCore 0:
  10.1 90.7 all-gather.1
  109.8 71.3 reduce-scatter.2
  183.7 33.7 reduce-scatter.4
where the time goes:
time: 226 us
  waiting for transfers between devices  202 us (89%)
  between operations  13.1 us (6%)
  matrix products  8.75 us (4%)
    reduce_scatter x2, waiting for transfers between devices, scatter_axes(): nearer = lax.psum_scatter(array, axes[0], scatter_dimension=dim, tiled=True)  108 us
    all_gather x1, waiting for transfers between devices, local(): lax.all_gather(grad_out, 'col', axis=0, tiled=True)  93.6 us
    dot_general x1, matrix products, contract(): lax.dot_general(rows_block, weight, (((1,), (1,)), ((), ())), preferred_e...  8.75 us
  transfers between devices with their start and end apart: 3, of which 3 were waited for; matrix products, arithmetic and copies ran while one was open for 0% of the time, Pallas kernels for 0%

commit v1 on v0

--- a/solution.py
+++ b/solution.py
@@ -21,7 +21,10 @@
 
 
 def local(grad_out, weight):
-    partial_value = contract(lax.all_gather(grad_out, "col", axis=0, tiled=True), weight)
+    measure_leaves = lambda u: jnp.concatenate(
+        lax.all_to_all(jnp.stack(lax.axis_size("col") * [u]), "col", 0, 0), axis=0
+    )
+    partial_value = contract(measure_leaves(grad_out), weight)
     return scatter_axes(partial_value, ROW, 0).astype(jnp.bfloat16)
 
 

time: 226 us -> 240 us (1.062)
  blocking collectives: 0 us -> 108 us
  waiting for transfers between devices: 202 us -> 108 us
    all_to_all x0 -> x1, blocking collectives: none -> 108 us  [local(): lax.all_to_all(jnp.stack(lax.axis_size('col') * [u]), 'col', 0, 0)]
    all_gather x1 -> x0, waiting for transfers between devices: 93.6 us -> none  [local(): lax.all_gather(grad_out, 'col', axis=0, tiled=True)]
  transfers between devices with their start and end apart: 3 -> 2, of which waited for: 3 -> 2; matrix products, arithmetic and copies ran while one was open for 0% -> 0% of each run, Pallas kernels for 0% -> 0%
where the time goes in v1:
time: 240 us
  blocking collectives  108 us (45%)
  waiting for transfers between devices  108 us (45%)
  between operations  13.4 us (6%)
  matrix products  6.59 us (3%)
    reduce_scatter x2, waiting for transfers between devices, scatter_axes(): nearer = lax.psum_scatter(array, axes[0], scatter_dimension=dim, tiled=True)  108 us
    all_to_all x1, blocking collectives, local(): lax.all_to_all(jnp.stack(lax.axis_size('col') * [u]), 'col', 0, 0)  108 us
    dot_general x1, matrix products, contract(): lax.dot_general(rows_block, weight, (((1,), (1,)), ((), ())), preferred_e...  6.59 us
  transfers between devices with their start and end apart: 2, of which 2 were waited for; matrix products, arithmetic and copies ran while one was open for 0% of the time, Pallas kernels for 0%

profile of v1, /device:TPU:1, one launch (start us, length us, event | category | flops | bytes accessed | tf_op | source)
XLA Modules:
  0.0 239.9 jit_solution(14339221556456197767)
XLA Ops:
  6.5 0.0 copy-start
  6.5 0.0 reduce-scatter.3.cloned.1.call-start
  6.5 1.6 stack.2
  8.1 108.0 %all_to_all.5 = bf16[32,64,1024]{2,1,0:T(8,128)(2,1)S(1)} all-to-all(bf16[32,64,1024]{2,1,0:T(8,128)(2,1)S(1)} %stack.2), channel_id=1, replica_groups=mesh['row_0'=4,'row_1'=2,'col'=32] {'col'}, dimensions={0} | all-to-all | bytes 8388608 | tf_op jit(solution)/shard_map/all_to_all | solution.py:25
  116.1 0.0 copy-done
  116.1 6.6 %fusion = f32[2048,896]{1,0:T(8,128)} fusion(bf16[2048,1024]{1,0:T(8,128)(2,1)S(1)} %bitcast.3, bf16[896,1024]{1,0:T(8,128)(2,1)S(1)} %copy-done), kind=kOutput, calls=%fused_computation | convolution fusion | flops 3758096384 | bytes 13369344 | tf_op jit(solution)/shard_map/dot_general | solution.py:18
  122.7 0.0 reduce-scatter.3.cloned.1.call-update
  122.7 0.0 reduce-scatter.5.cloned.1.call-start
  122.8 72.0 %reduce-scatter.3.cloned.1.call-done = f32[512,896]{1,0:T(8,128)} async-done(((f32[2048,896]{1,0:T(8,128)}), f32[512,896]{1,0:T(8,128)}) %reduce-scatter.3.cloned.1.call-update) | async-done | bytes 1835024 | tf_op jit(solution)/shard_map/reduce_scatter | solution.py:13
  194.8 0.0 reduce-scatter.5.cloned.1.call-update
  194.8 36.3 %reduce-scatter.5.cloned.1.call-done = f32[256,896]{1,0:T(8,128)} async-done(((f32[512,896]{1,0:T(8,128)}), f32[256,896]{1,0:T(8,128)}) %reduce-scatter.5.cloned.1.call-update) | async-done | bytes 917520 | tf_op jit(solution)/shard_map/reduce_scatter | solution.py:13
  231.1 2.0 convert_element_type.3
Async XLA Ops:
  6.5 109.6 %copy-start = (bf16[896,1024]{1,0:T(8,128)(2,1)S(1)}, bf16[896,1024]{1,0:T(8,128)(2,1)}, u32[]{:S(2)}) copy-start(bf16[896,1024]{1,0:T(8,128)(2,1)} %param.3) | copy-start | bytes 5505028
  6.5 188.3 %reduce-scatter.3.cloned.1.call-start = ((), (), s32[]{:S(2)}) async-start(), calls=%async_computation.3 | async-start | bytes 9175040 | tf_op jit(solution)/shard_map/reduce_scatter | solution.py:13
  122.7 108.4 %reduce-scatter.5.cloned.1.call-start = ((), (), s32[]{:S(2)}) async-start(), calls=%async_computation.4 | async-start | bytes 2752512 | tf_op jit(solution)/shard_map/reduce_scatter | solution.py:13
Sparse Core Ops, SparseCore 0:
  122.9 71.8 reduce-scatter.2
  197.3 33.7 reduce-scatter.4
